TPU v7x, 256 devices: a 4x2x16 block of a 4x16x16 slice. The times are simulated.
256 devices in a mesh: groups: 2 (over y), seq: 16 (over z), head: 8 (over x, core).
Axes of the slice: x: 4, y: 2, z: 16, core: 2. Of those that a mesh axis runs over, the one named last changes fastest.
The devices are a block of a 4x16x16 slice.
Arguments:
- residual: bfloat16 [16384, 2560], P(('groups', 'seq'), 'head'), parts along dimension 0, may hold values from -6 to 6
- x_in: bfloat16 [16384, 5120], P(('groups', 'seq'), 'head'), parts along dimension 0, may hold values from -6 to 6
- bc_in: bfloat16 [16384, 256], P(('groups', 'seq')), parts along dimension 0, may hold values from -1.5 to 1.5
- z_in: bfloat16 [16384, 5120], P(('groups', 'seq'), 'head'), parts along dimension 0, may hold values from -6 to 6
- dt_raw: float32 [80, 16384], P('head', ('groups', 'seq')), parts along dimension 1, may hold values from -5 to 5
- dt_bias: float32 [80], P('head'), may hold values from -3 to 0
- decay_rate: float32 [80], P('head'), may hold values from 0.0003 to 0.15
- d_skip: float32 [80], P('head'), may hold values from 1 to 4
- conv_x_weight: bfloat16 [4, 5120], P(None, 'head'), may hold values from -3 to 3
- conv_x_bias: bfloat16 [5120], P('head'), may hold values from -3 to 3
- conv_bc_weight: bfloat16 [4, 256], replicated, may hold values from -3 to 3
- conv_bc_bias: bfloat16 [256], replicated, may hold values from -3 to 3
- norm_gain: bfloat16 [5120], P('head'), may hold values from 0.5 to 1.5
- out_weight: bfloat16 [5120, 2560], P('head'), may hold values from -0.078125 to 0.078125
- final_gain: bfloat16 [2560], replicated, may hold values from 0.5 to 1.5
- lm_weight: bfloat16 [2560, 25600], P('seq', 'head'), may hold values from -15.811388 to 15.811388
- targets: int32 [16384], P(('groups', 'seq')), parts along dimension 0, may hold values from 0 to 25599
- doc_lengths: int32 [32], P('groups'), parts along dimension 0, may hold values from 1 to 1536, as said below
Outputs:
- block_out: bfloat16 [16384, 2560], P(('groups', 'seq'), 'head'), parts along dimension 0
- doc_loss: float32 [32], P('groups'), parts along dimension 0
There are 2 independent parts, one for each index of `groups`. A program takes and returns all parts, laid end to end along the dimension named above; an argument that names none is the same for every part. Nothing has to cross between parts.
Inputs may be any that keep to these rules, and one draw needn't show every extreme that they name: `doc_lengths`: the lengths of a group's 16 documents, in the order in which they are packed into its 8192 tokens; they sum to 8192.
All inputs are finite; a program needn't handle non-finite values.
Results may differ from a plain program's by a relative error of at most 0.00145.
The roundings to bfloat16 on the way count: a program that leaves them out, or rounds other values in their place, can miss the bound.
Values may be sent and summed in bfloat16 or wider, within the bound.
No kernel may reach another device: no remote copies, remote signals or barrier semaphores. Data moves between devices by JAX's collectives and lax.ppermute only.
A program may use at most 128 MiB of HBM per device.

v0:
```python
import jax
import jax.numpy as jnp
from jax import lax
from jax.sharding import PartitionSpec as P

D = 2560
HEAD_SIZE = 64
STATE = 128
KERNEL = 4
SPAN = 256
INNER = 5120
EPSILON = 1e-05
HIGH = lax.Precision.HIGHEST


def shifted(array, axis, by):
    length = lax.axis_size(axis)
    pairs = [(i, i + by) for i in range(length) if 0 <= i + by < length]
    return lax.ppermute(array, axis, pairs)


def entering(part, axis, combine, identity):
    place = lax.axis_index(axis)
    gathered = jax.tree.map(lambda a: lax.all_gather(a, axis), part)
    state = jax.tree.map(lambda a, e: jnp.zeros_like(a) + jnp.asarray(e, a.dtype), part, identity)

    def one(lap, state):
        return combine(
            state, jax.tree.map(lambda a: lax.dynamic_index_in_dim(a, lap, 0, False), gathered)
        )

    return lax.fori_loop(0, place, one, state)


def cut_along(array, dim, length):
    shape = array.shape
    blocks = array.reshape(*shape[:dim], length, shape[dim] // length, *shape[dim + 1 :])
    return jnp.moveaxis(blocks, dim, 0)


def sent_and_summed(array, axis, dim):
    blocks = cut_along(array, dim, lax.axis_size(axis))
    arrived = lax.all_to_all(blocks, axis, split_axis=0, concat_axis=0, tiled=True)
    return arrived.sum(axis=0)


def joined_along(blocks, dim):
    shape = list(blocks.shape[1:])
    shape[dim] *= blocks.shape[0]
    return jnp.moveaxis(blocks, 0, dim).reshape(shape)


def from_everyone(array, axis):
    length = lax.axis_size(axis)
    return lax.all_to_all(
        jnp.broadcast_to(array[None], (length, *array.shape)), axis, 0, 0, tiled=True
    )


def gather_directly(array, axis, dim):
    return joined_along(from_everyone(array, axis), dim)


def gathered_once(array, axis):
    leaves = jax.tree.leaves(array)
    sequence = sorted(range(len(leaves)), key=lambda k: -leaves[k].size)
    width = (1, *leaves[sequence[0]].shape)[-1]
    lines = [
        jnp.pad(leaves[k].reshape(-1), (0, -leaves[k].size % width)).reshape(-1, width)
        for k in sequence
    ]
    both, at, found = (lax.all_gather(jnp.concatenate(lines), axis), 0, {})
    for k, line in zip(sequence, lines):
        section = both[:, at : at + len(line)].reshape(len(both), -1)
        found[k] = section[:, : leaves[k].size].reshape(-1, *leaves[k].shape)
        at += len(line)
    numbers = iter(range(len(leaves)))
    return jax.tree.map(lambda _: found[next(numbers)], array)


def joined_2(part, axis, combine):
    gathered = gathered_once(part, axis)

    def take(source):
        return jax.tree.map(lambda a: lax.dynamic_index_in_dim(a, source, 0, False), gathered)

    return lax.fori_loop(
        1, lax.axis_size(axis), lambda source, state: combine(state, take(source)), take(0)
    )


def over_copies(array, axis):
    return from_everyone(array, axis).sum(axis=0)


def document_of(positions, doc_lengths):
    starts = jnp.cumsum(doc_lengths) - doc_lengths
    return jnp.sum((positions[:, None] >= starts[None, :]).astype(jnp.int32), axis=1) - 1


def causal_conv(signal, rim_rows, weight, bias, positions, doc_ids, doc_lengths):
    length = signal.shape[0]
    taps = weight.shape[0]
    joined = jnp.concatenate([rim_rows, signal], axis=0).astype(jnp.float32)
    total = jnp.zeros(signal.shape, jnp.float32) + bias.astype(jnp.float32)[None, :]
    for offset in range(taps):
        lag = taps - 1 - offset
        source = document_of(positions - lag, doc_lengths)
        same = (source == doc_ids).astype(jnp.float32)
        total = (
            total
            + weight[offset].astype(jnp.float32)[None, :]
            * joined[offset : offset + length]
            * same[:, None]
        )
    return jax.nn.silu(total).astype(jnp.bfloat16)


def span_step(state, pieces, rates):
    signal, bmat, cmat, steps, doc_ids, doc_prev = pieces
    signal = signal.astype(jnp.float32)
    bmat = bmat.astype(jnp.float32)
    cmat = cmat.astype(jnp.float32)
    climb = jnp.cumsum(steps * rates[:, None], axis=1)
    extent = doc_ids.shape[0]
    order = jnp.arange(extent, dtype=jnp.int32)
    inside = (doc_ids[:, None] == doc_ids[None, :]) & (order[:, None] >= order[None, :])
    gap = climb[:, :, None] - climb[:, None, :]
    decay = jnp.where(inside[None], jnp.exp(-jnp.where(inside[None], gap, 0.0)), 0.0)
    scores = jnp.dot(cmat, bmat.T, precision=HIGH)
    weights = decay * scores[None] * steps[:, None, :]
    output = jnp.einsum("hts,shp->thp", weights, signal, precision=HIGH)
    carried = (doc_ids == doc_prev).astype(jnp.float32)
    entry = jnp.exp(-climb) * carried[None, :]
    output = output + jnp.einsum("tn,hpn->thp", cmat, state, precision=HIGH) * entry.T[:, :, None]
    last = doc_ids[extent - 1]
    tail = (
        jnp.exp(climb - climb[:, extent - 1 :])
        * (doc_ids == last).astype(jnp.float32)[None, :]
        * steps
    )
    kept = jnp.exp(-climb[:, extent - 1]) * (last == doc_prev).astype(jnp.float32)
    fresh = jnp.einsum("hs,shp,sn->hpn", tail, signal, bmat, precision=HIGH)
    return (kept[:, None, None] * state + fresh, output)


def chain_combine(earlier, later):
    return (earlier[0] * later[0], later[0][:, None, None] * earlier[1] + later[1])


def softmax_combine(first_part, second_part):
    peak = jnp.maximum(first_part[0], second_part[0])
    total = first_part[1] * jnp.exp(first_part[0] - peak) + second_part[1] * jnp.exp(
        second_part[0] - peak
    )
    return (peak, total, first_part[2] + second_part[2])


def local(
    residual,
    x_in,
    bc_in,
    z_in,
    dt_raw,
    dt_bias,
    decay_rate,
    d_skip,
    conv_x_weight,
    conv_x_bias,
    conv_bc_weight,
    conv_bc_bias,
    norm_gain,
    out_weight,
    final_gain,
    lm_weight,
    targets,
    doc_lengths,
):
    length = x_in.shape[0]
    inner_here = x_in.shape[1]
    heads_here = dt_raw.shape[0]
    seq_rank = lax.axis_index("seq")
    head_rank = lax.axis_index("head")
    offset_here = seq_rank * length
    positions = offset_here + jnp.arange(length, dtype=jnp.int32)
    doc_ids = document_of(positions, doc_lengths)
    margin = KERNEL - 1
    x_rim, bc_rim = shifted((x_in[length - margin :], bc_in[length - margin :]), "seq", 1)
    signal = causal_conv(x_in, x_rim, conv_x_weight, conv_x_bias, positions, doc_ids, doc_lengths)
    keys_queries = causal_conv(
        bc_in, bc_rim, conv_bc_weight, conv_bc_bias, positions, doc_ids, doc_lengths
    )
    steps = jax.nn.softplus(dt_raw + dt_bias[:, None])
    blocks = length // SPAN
    block_starts = offset_here + jnp.arange(blocks, dtype=jnp.int32) * SPAN
    pieces = (
        signal.reshape(blocks, SPAN, heads_here, HEAD_SIZE),
        keys_queries[:, :STATE].reshape(blocks, SPAN, STATE),
        keys_queries[:, STATE:].reshape(blocks, SPAN, STATE),
        steps.reshape(heads_here, blocks, SPAN).transpose(1, 0, 2),
        doc_ids.reshape(blocks, SPAN),
        document_of(block_starts - 1, doc_lengths),
    )

    def advance(state, piece):
        return span_step(state, piece, decay_rate)

    local_end, outputs = lax.scan(
        advance, jnp.zeros((heads_here, HEAD_SIZE, STATE), jnp.float32), pieces
    )
    outputs = outputs.reshape(length, heads_here, HEAD_SIZE)
    before = document_of(jnp.reshape(offset_here - 1, (1,)), doc_lengths)[0]
    carried = (doc_ids == before).astype(jnp.float32)
    climb = jnp.cumsum(steps * decay_rate[:, None], axis=1)
    through = jnp.exp(-climb[:, length - 1]) * carried[length - 1]
    identity = (jnp.ones_like(through), jnp.zeros_like(local_end))
    incoming = entering((through, local_end), "seq", chain_combine, identity)[1]
    entry = jnp.exp(-climb) * carried[None, :]
    cmat = keys_queries[:, STATE:].astype(jnp.float32)
    outputs = (
        outputs + jnp.einsum("tn,hpn->thp", cmat, incoming, precision=HIGH) * entry.T[:, :, None]
    )
    mixed = outputs + d_skip[None, :, None] * signal.reshape(length, heads_here, HEAD_SIZE).astype(
        jnp.float32
    )
    gated = mixed.reshape(length, inner_here) * jax.nn.silu(z_in.astype(jnp.float32))
    square_sum = lax.psum(jnp.sum(gated * gated, axis=1), "head")
    scale = lax.rsqrt(square_sum / INNER + EPSILON)
    normed = (gated * scale[:, None] * norm_gain.astype(jnp.float32)[None, :]).astype(jnp.bfloat16)
    partial_value = jnp.dot(normed, out_weight, preferred_element_type=jnp.float32)
    share = residual.shape[1]
    projected = sent_and_summed(partial_value, "head", 1)
    block_out = (residual.astype(jnp.float32) + projected).astype(jnp.bfloat16)
    widened = block_out.astype(jnp.float32)
    square_total = lax.psum(jnp.sum(widened * widened, axis=1), "head")
    gain_part = lax.dynamic_slice_in_dim(final_gain, head_rank * share, share, 0)
    final_scale = lax.rsqrt(square_total / D + EPSILON)
    hidden_part = (widened * final_scale[:, None] * gain_part.astype(jnp.float32)[None, :]).astype(
        jnp.bfloat16
    )
    hidden = gather_directly(hidden_part, "head", 1)
    vocab_here = lm_weight.shape[1]
    logits = jnp.dot(
        hidden,
        lax.all_gather(lm_weight, "seq", axis=0, tiled=True),
        preferred_element_type=jnp.float32,
    )
    peak = jnp.max(logits, axis=1)
    total = jnp.sum(jnp.exp(logits - peak[:, None]), axis=1)
    local_target = targets - head_rank * vocab_here
    column = jnp.arange(vocab_here, dtype=jnp.int32)
    picked = jnp.sum(jnp.where(column[None, :] == local_target[:, None], logits, 0.0), axis=1)
    peak_all, total_all, picked_all = joined_2((peak, total, picked), "head", softmax_combine)
    losses = peak_all + jnp.log(total_all) - picked_all
    member = (
        doc_ids[:, None] == jnp.arange(doc_lengths.shape[0], dtype=jnp.int32)[None, :]
    ).astype(jnp.float32)
    sums = over_copies(jnp.dot(losses, member, precision=HIGH), "seq")
    return (block_out, sums / doc_lengths.astype(jnp.float32))


def solution(mesh):
    in_specs = (
        P(("groups", "seq"), "head"),
        P(("groups", "seq"), "head"),
        P(("groups", "seq"), None),
        P(("groups", "seq"), "head"),
        P("head", ("groups", "seq")),
        P("head"),
        P("head"),
        P("head"),
        P(None, "head"),
        P("head"),
        P(),
        P(),
        P("head"),
        P("head", None),
        P(),
        P("seq", "head"),
        P(("groups", "seq")),
        P("groups"),
    )
    out_specs = (P(("groups", "seq"), "head"), P("groups"))
    return jax.shard_map(local, mesh=mesh, in_specs=in_specs, out_specs=out_specs, check_vma=False)
```

profile of v0, /device:TPU:33, one launch (start us, length us, event | category | flops | bytes accessed | tf_op | source)
XLA Modules:
  0.0 454.0 jit_solution(4214907796771070101)
XLA Ops:
  8.7 5.8 %collective-permute-start = (bf16[3,640]{1,0:T(4,128)(2,1)}, bf16[3,640]{1,0:T(4,128)(2,1)}, u32[]{:S(2)}, u32[]{:S(2)}) collective-permute-start(bf16[3,640]{1,0:T(4,128)(2,1)} %slice.103), channel_id=1, source_target_pairs={{0,8},{8,16},{16,24},{24,32},{32,40},{40,48},{48,56},{56,64},{64,7... | collective-permute-start | bytes 11528 | tf_op jit(solution)/shard_map/ppermute | solution.py:19
  15.2 3.8 collective-permute-start.1
  41.5 80.0 %while.46 = (s32[]{:T(128)}, f32[10,64,128]{2,1,0:T(8,128)}, f32[2,256,10,64]{1,0,3,2:T(2,128)}, f32[2,10,256]{2,0,1:T(2,128)}, f32[10]{0:T(128)}, /*index=5*/s3...) while((s32[]{:T(128)}, f32[10,64,128]{2,1,0:T(8,128)}, ...), condition=%wide.region_9.10_spmd.clone, body=%wide.region_6.9_spmd.clone.sunk | while | flops 1028866112 | bytes 7581990 | solution.py:208
  51.7 4.0 fusion.117
  63.0 14.2 %dynamic_update_slice.6 = f32[2,256,10,64]{1,0,3,2:T(2,128)} dynamic-update-slice(f32[2,256,10,64]{1,0,3,2:T(2,128)} %get-tuple-element.624, f32[1,256,10,64]{1,0,3,2:T(1,128)} %copy.129, s32[]{:T(128)} %get-tuple-element.622, s32[]{:T(128)} %constant.152.clone.1..sunk.2, s32[]{:T(128)} %constant.152.clone.1..sunk.2, s32[]{:T(128)} %constant.152.clone.1..sunk.2) | dynamic-update-slice | bytes 1310724 | tf_op jit(solution)/shard_map/while/body/jit(dynamic_update_index_in_dim)/dynamic_update_slice | solution.py:208
  91.6 4.0 fusion.117
  103.0 14.2 %dynamic_update_slice.6 = f32[2,256,10,64]{1,0,3,2:T(2,128)} dynamic-update-slice(f32[2,256,10,64]{1,0,3,2:T(2,128)} %get-tuple-element.624, f32[1,256,10,64]{1,0,3,2:T(1,128)} %copy.129, s32[]{:T(128)} %get-tuple-element.622, s32[]{:T(128)} %constant.152.clone.1..sunk.2, s32[]{:T(128)} %constant.152.clone.1..sunk.2, s32[]{:T(128)} %constant.152.clone.1..sunk.2) | dynamic-update-slice | bytes 1310724 | tf_op jit(solution)/shard_map/while/body/jit(dynamic_update_index_in_dim)/dynamic_update_slice | solution.py:208
  126.8 39.9 %all-reduce = f32[160]{0:T(256)S(1)} all-reduce(f32[160]{0:T(256)S(1)} %dynamic-update-slice), channel_id=2, replica_groups=mesh['groups'=2,'seq'=16,'head'=8] {'seq'}, use_global_device_ids=true, to_apply=%add | all-reduce | flops 160 | bytes 1280
  169.8 3.2 reshape.296
  173.0 32.3 %all-gather.9.cloned.1.call-done = f32[160,64,128]{2,1,0:T(8,128)} async-done(((f32[10,64,128]{2,1,0:T(8,128)}), f32[160,64,128]{2,1,0:T(8,128)}) %all-gather.9.cloned.1.call-update) | async-done | bytes 5242896 | tf_op jit(solution)/shard_map/all_gather | solution.py:24
  207.0 3.7 fusion.46
  210.8 2.8 copy.90
  215.5 20.6 %psum.14 = f32[512]{0:T(512)S(1)} all-reduce(f32[512]{0:T(512)S(1)} %multiply_reduce_fusion), channel_id=1, replica_groups=mesh['groups'=2,'seq'=16,'head'=8] {'head'}, use_global_device_ids=true, to_apply=%region_16.17 | all-reduce | flops 512 | bytes 4096 | tf_op jit(solution)/shard_map/psum | solution.py:227
  236.2 6.4 %fusion.61 = f32[512,2560]{0,1:T(8,128)} fusion(bf16[640,2560]{1,0:T(8,128)(2,1)S(1)} %copy-done, f32[640]{0:T(1024)S(1)} %convert_element_type.158, f32[512]{0:T(512)S(1)} %add_rsqrt_fusion.1, f32[512,640]{1,0:T(8,128)} %copy.90, bf16[512,640]{1,0:T(8,128)(2,1)} %param.27), kind=kOutput, calls=%fused_computation.97 | convolution fusion | flops 1680670720 | bytes 10490368 | tf_op jit(solution)/shard_map/dot_general | solution.py:230
  242.5 5.2 %all-to-all-start = ((f32[8,512,320]{1,2,0:T(8,128)}), f32[8,512,320]{1,2,0:T(8,128)}, u32[]{:S(2)}, u32[]{:S(2)}) async-start(f32[8,512,320]{1,2,0:T(8,128)} %bitcast.151), calls=%async_computation | async-start | bytes 10485760 | tf_op jit(solution)/shard_map/all_to_all | solution.py:43
  248.5 59.3 %all-to-all-done = f32[8,512,320]{1,2,0:T(8,128)} async-done(((f32[8,512,320]{1,2,0:T(8,128)}), f32[8,512,320]{1,2,0:T(8,128)}, u32[]{:S(2)}, u32[]{:S(2)}) %all-to-all-start) | async-done | bytes 5242912 | tf_op jit(solution)/shard_map/all_to_all | solution.py:43
  307.9 4.0 reduce_sum.118
  313.9 13.2 %psum.15 = f32[512]{0:T(512)S(1)} all-reduce(f32[512]{0:T(512)S(1)} %get-tuple-element.424), channel_id=1, replica_groups=mesh['groups'=2,'seq'=16,'head'=8] {'head'}, use_global_device_ids=true, to_apply=%region_19.20 | all-reduce | flops 512 | bytes 4096 | tf_op jit(solution)/shard_map/psum | solution.py:235
  329.9 5.8 %all-to-all-start.1 = ((bf16[8,512,320]{1,2,0:T(8,128)(2,1)}), bf16[8,512,320]{1,2,0:T(8,128)(2,1)}, u32[]{:S(2)}, u32[]{:S(2)}) async-start(bf16[8,512,320]{1,2,0:T(8,128)(2,1)} %broadcast_in_dim.26), calls=%async_computation.1 | async-start | bytes 5242880 | tf_op jit(solution)/shard_map/all_to_all | solution.py:55
  335.7 32.0 %all-to-all-done.1 = bf16[8,512,320]{1,2,0:T(8,128)(2,1)} async-done(((bf16[8,512,320]{1,2,0:T(8,128)(2,1)}), bf16[8,512,320]{1,2,0:T(8,128)(2,1)}, u32[]{:S(2)}, u32[]{:S(2)}) %all-to-all-start.1) | async-done | bytes 2621472 | tf_op jit(solution)/shard_map/all_to_all | solution.py:55
  367.7 27.6 %all-gather.7.cloned.1.call-done = bf16[2560,3200]{1,0:T(8,128)(2,1)} async-done(((bf16[160,3200]{1,0:T(8,128)(2,1)}), bf16[2560,3200]{1,0:T(8,128)(2,1)}) %all-gather.7.cloned.1.call-update) | async-done | bytes 16384016 | tf_op jit(solution)/shard_map/all_gather | solution.py:245
  395.3 14.5 %fusion.89 = (f32[512]{0:T(512)S(1)}, f32[512,3200]{1,0:T(8,128)S(1)}) fusion(bf16[512,2560]{0,1:T(8,128)(2,1)} %bitcast.23, bf16[2560,3200]{1,0:T(8,128)(2,1)} %all-gather.7.cloned.1.call-done), kind=kOutput, calls=%fused_computation.170 | convolution fusion | flops 8390245888 | bytes 25561088 | tf_op jit(solution)/shard_map/dot_general | solution.py:243
  411.8 13.9 %all-gather.3 = f32[8,3,512]{2,1,0:T(4,128)S(1)} all-gather(f32[1,3,512]{2,1,0:T(4,128)S(1)} %maximum_bitcast_fusion), channel_id=4, replica_groups=mesh['groups'=2,'seq'=16,'head'=8] {'head'}, dimensions={0}, use_global_device_ids=true | all-gather | bytes 55296 | tf_op jit(solution)/shard_map/all_gather | solution.py:72
  426.8 19.8 %all_to_all.16 = f32[16,1,16]{2,1,0:T(1,128)S(1)} all-to-all(f32[16,1,16]{2,1,0:T(1,128)S(1)} %broadcast_in_dim.28), channel_id=1, replica_groups=mesh['groups'=2,'seq'=16,'head'=8] {'seq'}, dimensions={0} | all-to-all | bytes 2048 | tf_op jit(solution)/shard_map/all_to_all | solution.py:55
  (201 shorter events, 85.2 us)
Async XLA Ops:
  7.2 229.0 %copy-start = (bf16[640,2560]{1,0:T(8,128)(2,1)S(1)}, bf16[640,2560]{1,0:T(8,128)(2,1)}, u32[]{:S(2)}) copy-start(bf16[640,2560]{1,0:T(8,128)(2,1)} %param.37) | copy-start | bytes 9830404
  7.2 198.1 %all-gather.9.cloned.1.call-start = ((), (), s32[]{:S(2)}) async-start(), calls=%async_computation.4 | async-start | bytes 5570560 | tf_op jit(solution)/shard_map/all_gather | solution.py:24
  8.7 23.1 %collective-permute-start = (bf16[3,640]{1,0:T(4,128)(2,1)}, bf16[3,640]{1,0:T(4,128)(2,1)}, u32[]{:S(2)}, u32[]{:S(2)}) collective-permute-start(bf16[3,640]{1,0:T(4,128)(2,1)} %slice.103), channel_id=1, source_target_pairs={{0,8},{8,16},{16,24},{24,32},{32,40},{40,48},{48,56},{56,64},{64,7... | collective-permute-start | bytes 11528 | tf_op jit(solution)/shard_map/ppermute | solution.py:19
  15.2 14.4 %collective-permute-start.1 = (bf16[3,256]{1,0:T(4,128)(2,1)S(1)}, bf16[3,256]{1,0:T(4,128)(2,1)S(1)}, u32[]{:S(2)}, u32[]{:S(2)}) collective-permute-start(bf16[3,256]{1,0:T(4,128)(2,1)S(1)} %slice.112), channel_id=1, source_target_pairs={{0,8},{8,16},{16,24},{24,32},{32,40},{40,48},{48,56},{56,64},{64,7... | collective-permute-start | bytes 4616 | tf_op jit(solution)/shard_map/ppermute | solution.py:19
  22.9 7.7 %copy-start.13 = (s32[512]{0:T(512)}, s32[512]{0:T(512)S(1)}, u32[]{:S(2)}) copy-start(s32[512]{0:T(512)S(1)} %broadcast_add_fusion.2) | copy-start | bytes 6148
  31.1 1.5 copy-start.8
  31.1 1.5 copy-start.9
  31.1 1.5 copy-start.10
  31.1 1.5 copy-start.11
  48.3 3.4 copy-start.1
  58.6 1.4 copy-start.7
  61.5 17.7 %copy-start.2 = (f32[256,10]{0,1:T(8,128)S(1)}, f32[256,10]{0,1:T(8,128)}, u32[]{:S(2)}) copy-start(f32[256,10]{0,1:T(8,128)} %get-tuple-element.606) | copy-start | bytes 30724 | tf_op jit(solution)/shard_map/while
  88.1 3.4 copy-start.1
  98.5 1.4 copy-start.7
  101.5 17.7 %copy-start.2 = (f32[256,10]{0,1:T(8,128)S(1)}, f32[256,10]{0,1:T(8,128)}, u32[]{:S(2)}) copy-start(f32[256,10]{0,1:T(8,128)} %get-tuple-element.606) | copy-start | bytes 30724 | tf_op jit(solution)/shard_map/while
  121.4 1.5 copy-start.6
  121.4 3.0 copy-start.19
  121.4 45.3 %copy-start.15 = (bf16[640]{0:T(1024)(128)(2,1)S(1)}, bf16[640]{0:T(1024)(128)(2,1)}, u32[]{:S(2)}) copy-start(bf16[640]{0:T(1024)(128)(2,1)} %param.36) | copy-start | bytes 3844
  121.5 273.8 %all-gather.7.cloned.1.call-start = ((), (), s32[]{:S(2)}) async-start(), calls=%async_computation.3 | async-start | bytes 17408000 | tf_op jit(solution)/shard_map/all_gather | solution.py:245
  242.5 65.3 %all-to-all-start = ((f32[8,512,320]{1,2,0:T(8,128)}), f32[8,512,320]{1,2,0:T(8,128)}, u32[]{:S(2)}, u32[]{:S(2)}) async-start(f32[8,512,320]{1,2,0:T(8,128)} %bitcast.151), calls=%async_computation | async-start | bytes 10485760 | tf_op jit(solution)/shard_map/all_to_all | solution.py:43
  329.9 5.8 %copy-start.17 = (s32[512]{0:T(512)S(1)}, s32[512]{0:T(512)}, u32[]{:S(2)}) copy-start(s32[512]{0:T(512)} %param.40) | copy-start | bytes 6148
  329.9 37.8 %all-to-all-start.1 = ((bf16[8,512,320]{1,2,0:T(8,128)(2,1)}), bf16[8,512,320]{1,2,0:T(8,128)(2,1)}, u32[]{:S(2)}, u32[]{:S(2)}) async-start(bf16[8,512,320]{1,2,0:T(8,128)(2,1)} %broadcast_in_dim.26), calls=%async_computation.1 | async-start | bytes 5242880 | tf_op jit(solution)/shard_map/all_to_all | solution.py:55
  409.8 16.7 %copy-start.14 = (s32[512]{0:T(512)S(1)}, s32[512]{0:T(512)}, u32[]{:S(2)}) copy-start(s32[512]{0:T(512)} %copy-done.13) | copy-start | bytes 6148
  409.8 36.8 %copy-start.16 = (s32[16]{0:T(128)S(1)}, s32[16]{0:T(128)}, u32[]{:S(2)}) copy-start(s32[16]{0:T(128)} %param.41) | copy-start | bytes 196
  (5 other events, 4.6 us)
Sparse Core Ops, SparseCore 0:
  121.6 83.6 all-gather.8
  207.1 188.1 all-gather.6
where the time goes:
time: 458 us; the launch traced here: 454 us
  waiting for transfers between devices  152 us (33%)
  blocking collectives  107 us (23%)
  local copies, waits for them, and re-layouts  69.2 us (15%)
  other arithmetic  44.6 us (10%)
  matrix products  40.9 us (9%)
  starting transfers between devices  20.8 us (5%)
  between operations  15.8 us (3%)
    all_to_all x1, waiting for transfers between devices, sent_and_summed(): lax.all_to_all(blocks, axis, split_axis=0, concat_axis=0, tiled=True)  59.3 us
    unnamed x1, blocking collectives  39.9 us
    all_gather x1, waiting for transfers between devices, entering(): gathered = jax.tree.map(lambda a: lax.all_gather(a, axis), part)  32.3 us
    all_to_all x1, waiting for transfers between devices, from_everyone(): lax.all_to_all(jnp.broadcast_to(array[None], (length, *array.shape)), axi...  32 us
    dynamic_update_slice x4, local copies, waits for them, and re-layouts, local(): lax.scan(advance, jnp.zeros((heads_here, HEAD_SIZE, STATE), jnp.float32),...  31.3 us
    all_gather x1, waiting for transfers between devices, local(): lax.all_gather(lm_weight, 'seq', axis=0, tiled=True)  27.6 us
    psum x1, blocking collectives, local(): square_sum = lax.psum(jnp.sum(gated * gated, axis=1), 'head')  20.6 us
    all_to_all x1, blocking collectives, from_everyone(): lax.all_to_all(jnp.broadcast_to(array[None], (length, *array.shape)), axi...  19.8 us
  transfers between devices with their start and end apart: 6, of which 4 were waited for; matrix products, arithmetic and copies ran while one was open for 10% of the time, Pallas kernels for 0%

commit v1 on v0

--- a/solution.py
+++ b/solution.py
@@ -11,6 +11,19 @@
 INNER = 5120
 EPSILON = 1e-05
 HIGH = lax.Precision.HIGHEST
+
+
+def ring_gather(x, axis, dim):
+    ways = lax.axis_size(axis)
+    up = [(d, (d + 1) % ways) for d in range(ways)]
+    down = [(d, (d - 1) % ways) for d in range(ways)]
+    earlier, later = ([x], [x])
+    for _ in range(ways // 2):
+        earlier.append(lax.ppermute(earlier[-1], axis, up))
+    for _ in range((ways - 1) // 2):
+        later.append(lax.ppermute(later[-1], axis, down))
+    line = jnp.concatenate([*earlier[::-1], *later[1:]], axis=dim)
+    return jnp.roll(line, (lax.axis_index(axis) - ways // 2) * x.shape[dim], axis=dim)
 
 
 def shifted(array, axis, by):
@@ -240,11 +253,7 @@
     )
     hidden = gather_directly(hidden_part, "head", 1)
     vocab_here = lm_weight.shape[1]
-    logits = jnp.dot(
-        hidden,
-        lax.all_gather(lm_weight, "seq", axis=0, tiled=True),
-        preferred_element_type=jnp.float32,
-    )
+    logits = jnp.dot(hidden, ring_gather(lm_weight, "seq", 0), preferred_element_type=jnp.float32)
     peak = jnp.max(logits, axis=1)
     total = jnp.sum(jnp.exp(logits - peak[:, None]), axis=1)
     local_target = targets - head_rank * vocab_here

time: 458 us -> 603 us (1.32)
  the two profiles are of different devices: /device:TPU:33 before, /device:TPU:40 now
where the time goes in v1:
time: 603 us; the launch traced here: 591 us
  waiting for transfers between devices  181 us (30%)
  local copies, waits for them, and re-layouts  136 us (23%)
  blocking collectives  133 us (22%)
  other arithmetic  43.3 us (7%)
  matrix products  41.3 us (7%)
  starting transfers between devices  38 us (6%)
  between operations  15.9 us (3%)
    ppermute x8, waiting for transfers between devices, ring_gather(): earlier.append(lax.ppermute(earlier[-1], axis, up))  117 us
    unnamed x80, local copies, waits for them, and re-layouts  69.6 us
    unnamed x1, blocking collectives  51.9 us
    all_to_all x1, blocking collectives, from_everyone(): lax.all_to_all(jnp.broadcast_to(array[None], (length, *array.shape)), axi...  42.2 us
    all_to_all x1, waiting for transfers between devices, sent_and_summed(): lax.all_to_all(blocks, axis, split_axis=0, concat_axis=0, tiled=True)  41.4 us
    dynamic_update_slice x4, local copies, waits for them, and re-layouts, local(): lax.scan(advance, jnp.zeros((heads_here, HEAD_SIZE, STATE), jnp.float32),...  31.4 us
    all_to_all x1, waiting for transfers between devices, from_everyone(): lax.all_to_all(jnp.broadcast_to(array[None], (length, *array.shape)), axi...  22.6 us
    ppermute x7, starting transfers between devices, ring_gather(): later.append(lax.ppermute(later[-1], axis, down))  21.6 us
  transfers between devices with their start and end apart: 20, of which 8 were waited for; matrix products, arithmetic and copies ran while one was open for 30% of the time, Pallas kernels for 0%

profile of v1, /device:TPU:40, one launch (start us, length us, event | category | flops | bytes accessed | tf_op | source)
XLA Modules:
  0.0 591.2 jit_solution(16166351554593533153)
XLA Ops:
  10.2 42.5 %collective-permute-done.2 = bf16[160,3200]{1,0:T(8,128)(2,1)S(1)} collective-permute-done((bf16[160,3200]{1,0:T(8,128)(2,1)}, bf16[160,3200]{1,0:T(8,128)(2,1)S(1)}, u32[]{:S(2)}, u32[]{:S(2)}) %collective-permute-start.2) | collective-permute-done | bytes 1024032 | tf_op jit(solution)/shard_map/ppermute | solution.py:22
  56.9 21.8 %collective-permute-done.3 = bf16[160,3200]{1,0:T(8,128)(2,1)S(1)} collective-permute-done((bf16[160,3200]{1,0:T(8,128)(2,1)S(1)}, bf16[160,3200]{1,0:T(8,128)(2,1)S(1)}, u32[]{:S(2)}, u32[]{:S(2)}) %collective-permute-start.3) | collective-permute-done | bytes 1024032 | tf_op jit(solution)/shard_map/ppermute | solution.py:22
  83.0 21.1 %collective-permute-done.4 = bf16[160,3200]{1,0:T(8,128)(2,1)} collective-permute-done((bf16[160,3200]{1,0:T(8,128)(2,1)S(1)}, bf16[160,3200]{1,0:T(8,128)(2,1)}, u32[]{:S(2)}, u32[]{:S(2)}) %collective-permute-start.4) | collective-permute-done | bytes 1024032 | tf_op jit(solution)/shard_map/ppermute | solution.py:22
  114.6 13.2 %collective-permute-done.5 = bf16[160,3200]{1,0:T(8,128)(2,1)} collective-permute-done((bf16[160,3200]{1,0:T(8,128)(2,1)}, bf16[160,3200]{1,0:T(8,128)(2,1)}, u32[]{:S(2)}, u32[]{:S(2)}) %collective-permute-start.5) | collective-permute-done | bytes 1024032 | tf_op jit(solution)/shard_map/ppermute | solution.py:22
  140.1 10.4 %collective-permute-done.6 = bf16[160,3200]{1,0:T(8,128)(2,1)} collective-permute-done((bf16[160,3200]{1,0:T(8,128)(2,1)}, bf16[160,3200]{1,0:T(8,128)(2,1)}, u32[]{:S(2)}, u32[]{:S(2)}) %collective-permute-start.6) | collective-permute-done | bytes 1024032 | tf_op jit(solution)/shard_map/ppermute | solution.py:22
  166.1 7.7 %collective-permute-done.7 = bf16[160,3200]{1,0:T(8,128)(2,1)} collective-permute-done((bf16[160,3200]{1,0:T(8,128)(2,1)}, bf16[160,3200]{1,0:T(8,128)(2,1)}, u32[]{:S(2)}, u32[]{:S(2)}) %collective-permute-start.7) | collective-permute-done | bytes 1024032 | tf_op jit(solution)/shard_map/ppermute | solution.py:22
  173.8 78.4 %while.46 = (s32[]{:T(128)}, f32[10,64,128]{2,1,0:T(8,128)}, f32[2,256,10,64]{1,0,3,2:T(2,128)}, f32[2,10,256]{2,0,1:T(2,128)}, f32[10]{0:T(128)}, /*index=5*/s3...) while((s32[]{:T(128)}, f32[10,64,128]{2,1,0:T(8,128)}, ...), condition=%wide.region_9.10_spmd.clone, body=%wide.region_6.9_spmd.clone.sunk | while | flops 1028866112 | bytes 7540814 | solution.py:221
  184.0 4.1 fusion.119
  195.3 14.2 %dynamic_update_slice.6 = f32[2,256,10,64]{1,0,3,2:T(2,128)} dynamic-update-slice(f32[2,256,10,64]{1,0,3,2:T(2,128)} %get-tuple-element.624, f32[1,256,10,64]{1,0,3,2:T(1,128)} %copy.129, s32[]{:T(128)} %get-tuple-element.622, s32[]{:T(128)} %constant.171.clone.1..sunk.2, s32[]{:T(128)} %constant.171.clone.1..sunk.2, s32[]{:T(128)} %constant.171.clone.1..sunk.2) | dynamic-update-slice | bytes 1310724 | tf_op jit(solution)/shard_map/while/body/jit(dynamic_update_index_in_dim)/dynamic_update_slice | solution.py:221
  223.1 4.1 fusion.119
  234.5 14.2 %dynamic_update_slice.6 = f32[2,256,10,64]{1,0,3,2:T(2,128)} dynamic-update-slice(f32[2,256,10,64]{1,0,3,2:T(2,128)} %get-tuple-element.624, f32[1,256,10,64]{1,0,3,2:T(1,128)} %copy.129, s32[]{:T(128)} %get-tuple-element.622, s32[]{:T(128)} %constant.171.clone.1..sunk.2, s32[]{:T(128)} %constant.171.clone.1..sunk.2, s32[]{:T(128)} %constant.171.clone.1..sunk.2) | dynamic-update-slice | bytes 1310724 | tf_op jit(solution)/shard_map/while/body/jit(dynamic_update_index_in_dim)/dynamic_update_slice | solution.py:221
  252.3 3.4 collective-permute-start.15
  262.0 51.9 %all-reduce = f32[160]{0:T(256)S(1)} all-reduce(f32[160]{0:T(256)S(1)} %dynamic-update-slice), channel_id=2, replica_groups=mesh['groups'=2,'seq'=16,'head'=8] {'seq'}, use_global_device_ids=true, to_apply=%add | all-reduce | flops 160 | bytes 1280
  361.7 3.7 fusion.48
  370.1 12.8 %psum.14 = f32[512]{0:T(512)S(1)} all-reduce(f32[512]{0:T(512)S(1)} %multiply_reduce_fusion), channel_id=1, replica_groups=mesh['groups'=2,'seq'=16,'head'=8] {'head'}, use_global_device_ids=true, to_apply=%region_16.17 | all-reduce | flops 512 | bytes 4096 | tf_op jit(solution)/shard_map/psum | solution.py:240
  383.0 6.4 %fusion.63 = f32[512,2560]{0,1:T(8,128)} fusion(bf16[640,2560]{1,0:T(8,128)(2,1)S(1)} %copy-done, f32[640]{0:T(1024)S(1)} %copy-done.19, f32[512]{0:T(512)S(1)} %add_rsqrt_fusion.1, f32[512,640]{1,0:T(8,128)} %copy.90, bf16[512,640]{1,0:T(8,128)(2,1)} %param.27), kind=kOutput, calls=%fused_computation.99 | convolution fusion | flops 1680670720 | bytes 10490368 | tf_op jit(solution)/shard_map/dot_general | solution.py:243
  389.4 4.8 all-to-all-start
  413.6 41.4 %all-to-all-done = f32[8,512,320]{1,2,0:T(8,128)} async-done(((f32[8,512,320]{1,2,0:T(8,128)}), f32[8,512,320]{1,2,0:T(8,128)}, u32[]{:S(2)}, u32[]{:S(2)}) %all-to-all-start) | async-done | bytes 5242912 | tf_op jit(solution)/shard_map/all_to_all | solution.py:56
  458.3 12.7 %psum.15 = f32[512]{0:T(512)S(1)} all-reduce(f32[512]{0:T(512)S(1)} %get-tuple-element.424), channel_id=1, replica_groups=mesh['groups'=2,'seq'=16,'head'=8] {'head'}, use_global_device_ids=true, to_apply=%region_19.20 | all-reduce | flops 512 | bytes 4096 | tf_op jit(solution)/shard_map/psum | solution.py:248
  472.9 4.9 all-to-all-start.1
  488.0 22.6 %all-to-all-done.1 = bf16[8,512,320]{1,2,0:T(8,128)(2,1)} async-done(((bf16[8,512,320]{1,2,0:T(8,128)(2,1)}), bf16[8,512,320]{1,2,0:T(8,128)(2,1)}, u32[]{:S(2)}, u32[]{:S(2)}) %all-to-all-start.1) | async-done | bytes 2621472 | tf_op jit(solution)/shard_map/all_to_all | solution.py:68
  510.6 14.8 %fusion.92 = (f32[512]{0:T(512)S(1)}, f32[512,3200]{1,0:T(8,128)S(1)}) fusion(bf16[512,2560]{0,1:T(8,128)(2,1)} %bitcast.23, bf16[5120,3200]{1,0:T(8,128)(2,1)} %constant_dynamic-update-slice_fusion, s32[]{:T(128)S(6)} %select_n.57), kind=kOutput, calls=%fused_computation.205 | convolution fusion | flops 8390245888 | bytes 25561092 | tf_op jit(solution)/shard_map/dot_general | solution.py:256
  527.4 12.9 %all-gather.3 = f32[8,3,512]{2,1,0:T(4,128)S(1)} all-gather(f32[1,3,512]{2,1,0:T(4,128)S(1)} %maximum_bitcast_fusion), channel_id=4, replica_groups=mesh['groups'=2,'seq'=16,'head'=8] {'head'}, dimensions={0}, use_global_device_ids=true | all-gather | bytes 55296 | tf_op jit(solution)/shard_map/all_gather | solution.py:85
  541.4 42.2 %all_to_all.16 = f32[16,1,16]{2,1,0:T(1,128)S(1)} all-to-all(f32[16,1,16]{2,1,0:T(1,128)S(1)} %broadcast_in_dim.28), channel_id=1, replica_groups=mesh['groups'=2,'seq'=16,'head'=8] {'seq'}, dimensions={0} | all-to-all | bytes 2048 | tf_op jit(solution)/shard_map/all_to_all | solution.py:68
  (258 shorter events, 185.3 us)
Async XLA Ops:
  7.2 375.8 %copy-start = (bf16[640,2560]{1,0:T(8,128)(2,1)S(1)}, bf16[640,2560]{1,0:T(8,128)(2,1)}, u32[]{:S(2)}) copy-start(bf16[640,2560]{1,0:T(8,128)(2,1)} %param.37) | copy-start | bytes 9830404
  7.2 353.7 %all-gather.6.cloned.1.call-start = ((), (), s32[]{:S(2)}) async-start(), calls=%async_computation.3 | async-start | bytes 5570560 | tf_op jit(solution)/shard_map/all_gather | solution.py:37
  7.3 45.4 %collective-permute-start.2 = (bf16[160,3200]{1,0:T(8,128)(2,1)}, bf16[160,3200]{1,0:T(8,128)(2,1)S(1)}, u32[]{:S(2)}, u32[]{:S(2)}) collective-permute-start(bf16[160,3200]{1,0:T(8,128)(2,1)} %param.39), channel_id=1, source_target_pairs={{0,8},{8,16},{16,24},{24,32},{32,40},{40,48},{48,56},{56,64},{64,7... | collective-permute-start | bytes 3072008 | tf_op jit(solution)/shard_map/ppermute | solution.py:22
  53.7 25.1 %collective-permute-start.3 = (bf16[160,3200]{1,0:T(8,128)(2,1)S(1)}, bf16[160,3200]{1,0:T(8,128)(2,1)S(1)}, u32[]{:S(2)}, u32[]{:S(2)}) collective-permute-start(bf16[160,3200]{1,0:T(8,128)(2,1)S(1)} %collective-permute-done.2), channel_id=1, source_target_pairs={{0,8},{8,16},{16,24},{24,32},{32,40},{40,48},{48,56},{56,64},{64,7... | collective-permute-start | bytes 3072008 | tf_op jit(solution)/shard_map/ppermute | solution.py:22
  53.7 26.1 %collective-permute-start.10 = (bf16[160,3200]{1,0:T(8,128)(2,1)}, bf16[160,3200]{1,0:T(8,128)(2,1)}, u32[]{:S(2)}, u32[]{:S(2)}) collective-permute-start(bf16[160,3200]{1,0:T(8,128)(2,1)} %param.39), channel_id=1, source_target_pairs={{0,120},{8,0},{16,8},{24,16},{32,24},{40,32},{48,40},{56,48},{64,5... | collective-permute-start | bytes 3072008 | tf_op jit(solution)/shard_map/ppermute | solution.py:24
  79.7 24.3 %collective-permute-start.4 = (bf16[160,3200]{1,0:T(8,128)(2,1)S(1)}, bf16[160,3200]{1,0:T(8,128)(2,1)}, u32[]{:S(2)}, u32[]{:S(2)}) collective-permute-start(bf16[160,3200]{1,0:T(8,128)(2,1)S(1)} %collective-permute-done.3), channel_id=1, source_target_pairs={{0,8},{8,16},{16,24},{24,32},{32,40},{40,48},{48,56},{56,64},{64,7... | collective-permute-start | bytes 3072008 | tf_op jit(solution)/shard_map/ppermute | solution.py:22
  79.7 32.0 %collective-permute-start.11 = (bf16[160,3200]{1,0:T(8,128)(2,1)}, bf16[160,3200]{1,0:T(8,128)(2,1)}, u32[]{:S(2)}, u32[]{:S(2)}) collective-permute-start(bf16[160,3200]{1,0:T(8,128)(2,1)} %collective-permute-done.10), channel_id=1, source_target_pairs={{0,120},{8,0},{16,8},{24,16},{32,24},{40,32},{48,40},{56,48},{64,5... | collective-permute-start | bytes 3072008 | tf_op jit(solution)/shard_map/ppermute | solution.py:24
  104.1 23.7 %collective-permute-start.5 = (bf16[160,3200]{1,0:T(8,128)(2,1)}, bf16[160,3200]{1,0:T(8,128)(2,1)}, u32[]{:S(2)}, u32[]{:S(2)}) collective-permute-start(bf16[160,3200]{1,0:T(8,128)(2,1)} %collective-permute-done.4), channel_id=1, source_target_pairs={{0,8},{8,16},{16,24},{24,32},{32,40},{40,48},{48,56},{56,64},{64,7... | collective-permute-start | bytes 3072008 | tf_op jit(solution)/shard_map/ppermute | solution.py:22
  105.4 46.8 %collective-permute-start = (bf16[3,640]{1,0:T(4,128)(2,1)}, bf16[3,640]{1,0:T(4,128)(2,1)}, u32[]{:S(2)}, u32[]{:S(2)}) collective-permute-start(bf16[3,640]{1,0:T(4,128)(2,1)} %slice.103), channel_id=1, source_target_pairs={{0,8},{8,16},{16,24},{24,32},{32,40},{40,48},{48,56},{56,64},{64,7... | collective-permute-start | bytes 11528 | tf_op jit(solution)/shard_map/ppermute | solution.py:32
  107.9 27.8 %collective-permute-start.1 = (bf16[3,256]{1,0:T(4,128)(2,1)S(1)}, bf16[3,256]{1,0:T(4,128)(2,1)S(1)}, u32[]{:S(2)}, u32[]{:S(2)}) collective-permute-start(bf16[3,256]{1,0:T(4,128)(2,1)S(1)} %slice.112), channel_id=1, source_target_pairs={{0,8},{8,16},{16,24},{24,32},{32,40},{40,48},{48,56},{56,64},{64,7... | collective-permute-start | bytes 4616 | tf_op jit(solution)/shard_map/ppermute | solution.py:32
  111.8 25.0 %collective-permute-start.12 = (bf16[160,3200]{1,0:T(8,128)(2,1)}, bf16[160,3200]{1,0:T(8,128)(2,1)}, u32[]{:S(2)}, u32[]{:S(2)}) collective-permute-start(bf16[160,3200]{1,0:T(8,128)(2,1)} %collective-permute-done.11), channel_id=1, source_target_pairs={{0,120},{8,0},{16,8},{24,16},{32,24},{40,32},{48,40},{56,48},{64,5... | collective-permute-start | bytes 3072008 | tf_op jit(solution)/shard_map/ppermute | solution.py:24
  127.7 22.8 %collective-permute-start.6 = (bf16[160,3200]{1,0:T(8,128)(2,1)}, bf16[160,3200]{1,0:T(8,128)(2,1)}, u32[]{:S(2)}, u32[]{:S(2)}) collective-permute-start(bf16[160,3200]{1,0:T(8,128)(2,1)} %collective-permute-done.5), channel_id=1, source_target_pairs={{0,8},{8,16},{16,24},{24,32},{32,40},{40,48},{48,56},{56,64},{64,7... | collective-permute-start | bytes 3072008 | tf_op jit(solution)/shard_map/ppermute | solution.py:22
  136.8 26.1 %collective-permute-start.13 = (bf16[160,3200]{1,0:T(8,128)(2,1)}, bf16[160,3200]{1,0:T(8,128)(2,1)}, u32[]{:S(2)}, u32[]{:S(2)}) collective-permute-start(bf16[160,3200]{1,0:T(8,128)(2,1)} %collective-permute-done.12), channel_id=1, source_target_pairs={{0,120},{8,0},{16,8},{24,16},{32,24},{40,32},{48,40},{56,48},{64,5... | collective-permute-start | bytes 3072008 | tf_op jit(solution)/shard_map/ppermute | solution.py:24
  150.6 23.3 %collective-permute-start.7 = (bf16[160,3200]{1,0:T(8,128)(2,1)}, bf16[160,3200]{1,0:T(8,128)(2,1)}, u32[]{:S(2)}, u32[]{:S(2)}) collective-permute-start(bf16[160,3200]{1,0:T(8,128)(2,1)} %collective-permute-done.6), channel_id=1, source_target_pairs={{0,8},{8,16},{16,24},{24,32},{32,40},{40,48},{48,56},{56,64},{64,7... | collective-permute-start | bytes 3072008 | tf_op jit(solution)/shard_map/ppermute | solution.py:22
  162.9 89.4 %collective-permute-start.14 = (bf16[160,3200]{1,0:T(8,128)(2,1)}, bf16[160,3200]{1,0:T(8,128)(2,1)}, u32[]{:S(2)}, u32[]{:S(2)}) collective-permute-start(bf16[160,3200]{1,0:T(8,128)(2,1)} %collective-permute-done.13), channel_id=1, source_target_pairs={{0,120},{8,0},{16,8},{24,16},{32,24},{40,32},{48,40},{56,48},{64,5... | collective-permute-start | bytes 3072008 | tf_op jit(solution)/shard_map/ppermute | solution.py:24
  173.8 81.8 %collective-permute-start.8 = (bf16[160,3200]{1,0:T(8,128)(2,1)}, bf16[160,3200]{1,0:T(8,128)(2,1)}, u32[]{:S(2)}, u32[]{:S(2)}) collective-permute-start(bf16[160,3200]{1,0:T(8,128)(2,1)} %collective-permute-done.7), channel_id=1, source_target_pairs={{0,8},{8,16},{16,24},{24,32},{32,40},{40,48},{48,56},{56,64},{64,7... | collective-permute-start | bytes 3072008 | tf_op jit(solution)/shard_map/ppermute | solution.py:22
  252.3 71.3 %collective-permute-start.15 = (bf16[160,3200]{1,0:T(8,128)(2,1)}, bf16[160,3200]{1,0:T(8,128)(2,1)}, u32[]{:S(2)}, u32[]{:S(2)}) collective-permute-start(bf16[160,3200]{1,0:T(8,128)(2,1)} %collective-permute-done.14), channel_id=1, source_target_pairs={{0,120},{8,0},{16,8},{24,16},{32,24},{40,32},{48,40},{56,48},{64,5... | collective-permute-start | bytes 3072008 | tf_op jit(solution)/shard_map/ppermute | solution.py:24
  255.6 70.4 %collective-permute-start.9 = (bf16[160,3200]{1,0:T(8,128)(2,1)}, bf16[160,3200]{1,0:T(8,128)(2,1)}, u32[]{:S(2)}, u32[]{:S(2)}) collective-permute-start(bf16[160,3200]{1,0:T(8,128)(2,1)} %collective-permute-done.8), channel_id=1, source_target_pairs={{0,8},{8,16},{16,24},{24,32},{32,40},{40,48},{48,56},{56,64},{64,7... | collective-permute-start | bytes 3072008 | tf_op jit(solution)/shard_map/ppermute | solution.py:22
  323.5 33.1 %collective-permute-start.16 = (bf16[160,3200]{1,0:T(8,128)(2,1)}, bf16[160,3200]{1,0:T(8,128)(2,1)S(1)}, u32[]{:S(2)}, u32[]{:S(2)}) collective-permute-start(bf16[160,3200]{1,0:T(8,128)(2,1)} %collective-permute-done.15), channel_id=1, source_target_pairs={{0,120},{8,0},{16,8},{24,16},{32,24},{40,32},{48,40},{56,48},{64,5... | collective-permute-start | bytes 3072008 | tf_op jit(solution)/shard_map/ppermute | solution.py:24
  389.4 65.6 %all-to-all-start = ((f32[8,512,320]{1,2,0:T(8,128)}), f32[8,512,320]{1,2,0:T(8,128)}, u32[]{:S(2)}, u32[]{:S(2)}) async-start(f32[8,512,320]{1,2,0:T(8,128)} %bitcast.150), calls=%async_computation | async-start | bytes 10485760 | tf_op jit(solution)/shard_map/all_to_all | solution.py:56
  406.8 51.3 %copy-start.16 = (bf16[512,320]{0,1:T(8,128)(2,1)S(1)}, bf16[512,320]{0,1:T(8,128)(2,1)}, u32[]{:S(2)}) copy-start(bf16[512,320]{0,1:T(8,128)(2,1)} %param.24) | copy-start | bytes 983044
  472.9 37.6 %all-to-all-start.1 = ((bf16[8,512,320]{1,2,0:T(8,128)(2,1)}), bf16[8,512,320]{1,2,0:T(8,128)(2,1)}, u32[]{:S(2)}, u32[]{:S(2)}) async-start(bf16[8,512,320]{1,2,0:T(8,128)(2,1)} %broadcast_in_dim.26), calls=%async_computation.1 | async-start | bytes 5242880 | tf_op jit(solution)/shard_map/all_to_all | solution.py:68
  510.6 73.6 %copy-start.1 = (bf16[640,2560]{1,0:T(8,128)(2,1)S(1)}, bf16[640,2560]{1,0:T(8,128)(2,1)}, u32[]{:S(2)}) copy-start(bf16[640,2560]{1,0:T(8,128)(2,1)} %param.37) | copy-start | bytes 9830404
  525.4 58.2 %copy-start.20 = (s32[16]{0:T(128)S(1)}, s32[16]{0:T(128)}, u32[]{:S(2)}) copy-start(s32[16]{0:T(128)} %param.41) | copy-start | bytes 196
  (18 other events, 198.4 us)
Sparse Core Ops, SparseCore 0:
  252.4 92.0 all-gather.5
